TPU v7x, 32 devices: a whole 2x2x4 slice. The times are simulated.
32 devices in a mesh: dp: 2 (over x), tp: 16 (over z, y, core).
Axes of the slice: x: 2, y: 2, z: 4, core: 2. Of those that a mesh axis runs over, the one named last changes fastest.
Arguments:
- hidden: bfloat16 [2, 2048, 4096], P('dp'), parts along dimension 0
- grad_out: bfloat16 [2, 2048, 4096], P('dp'), parts along dimension 0
- norm_gain: bfloat16 [4096], replicated
- w_query: bfloat16 [4096, 4096], P(None, 'tp')
- w_key: bfloat16 [4096, 1024], replicated
- w_value: bfloat16 [4096, 1024], replicated
- w_out: bfloat16 [4096, 4096], P('tp')
Outputs:
- output 1: bfloat16 [2, 2048, 4096], P('dp'), parts along dimension 0
- output 2: bfloat16 [2, 2048, 4096], P('dp'), parts along dimension 0
- output 3: float32 [8192], P('dp'), parts along dimension 0
- output 4: float32 [8192, 4096], P('dp', 'tp'), parts along dimension 0
- output 5: float32 [8192, 2048], P('dp', 'tp'), parts along dimension 0
- output 6: float32 [8192, 2048], P('dp', 'tp'), parts along dimension 0
- output 7: float32 [8192, 4096], P(('dp', 'tp')), parts along dimension 0
There are 2 independent parts. A program takes and returns all parts, laid end to end along the dimension named above; an argument that names none is the same for every part.
All inputs are finite; a program needn't handle non-finite values.
Results may differ from a plain program's by a relative error of at most 0.00980688.
Values sent between devices are 32-bit elements.
A program may use at most 1 GiB of HBM per device.

v0:
```python
import math
import jax
import jax.numpy as jnp
from jax import lax
from jax.sharding import PartitionSpec as P

HEAD_DIM = 128
NORM_EPS = 1.0e-5
ROPE_BASE = 10000.0
MASK_VALUE = -1.0e30
SCORE_SCALE = 1.0 / math.sqrt(HEAD_DIM)


def rope_tables(seq_len):
    positions = jnp.arange(seq_len, dtype=jnp.float32)
    inv_freq = ROPE_BASE ** (-jnp.arange(0, HEAD_DIM, 2, dtype=jnp.float32) / HEAD_DIM)
    angles = positions[:, None] * inv_freq[None, :]
    return jnp.cos(angles), jnp.sin(angles)


def rotate_pairs(tensor, cos_t, sin_t):
    pair_view = tensor.reshape(tensor.shape[:-1] + (HEAD_DIM // 2, 2))
    even_part = pair_view[..., 0]
    odd_part = pair_view[..., 1]
    cos_b = cos_t[:, None, :]
    sin_b = sin_t[:, None, :]
    rotated = jnp.stack([even_part * cos_b - odd_part * sin_b, even_part * sin_b + odd_part * cos_b], axis=-1)
    return rotated.reshape(tensor.shape)


def group_sum(tensor, tp_size, group_size):
    total = tensor
    for level in range(group_size.bit_length() - 1):
        distance = 2 ** level
        partner_pairs = [(source, source ^ distance) for source in range(tp_size)]
        total = total + lax.ppermute(total, 'tp', perm=partner_pairs)
    return total


def solution(mesh):
    tp_size = mesh.shape['tp']

    def block_fn(hidden, grad_out, norm_gain, w_query, w_key, w_value, w_out):
        kv_heads = w_key.shape[1] // HEAD_DIM
        group_size = tp_size // kv_heads
        q_heads_local = w_query.shape[1] // HEAD_DIM
        batch_local, seq_len, d_model = hidden.shape
        kv_index = lax.axis_index('tp') // group_size
        w_kv = jnp.concatenate([
            lax.dynamic_slice_in_dim(w_key, kv_index * HEAD_DIM, HEAD_DIM, axis=1),
            lax.dynamic_slice_in_dim(w_value, kv_index * HEAD_DIM, HEAD_DIM, axis=1)], axis=1)
        cos_t, sin_t = rope_tables(seq_len)

        hidden_f32 = hidden.astype(jnp.float32)
        inv_rms = lax.rsqrt(jnp.mean(hidden_f32 * hidden_f32, axis=-1, keepdims=True) + NORM_EPS)
        unit_rows = hidden_f32 * inv_rms
        gain_f32 = norm_gain.astype(jnp.float32)
        normed = (unit_rows * gain_f32).astype(jnp.bfloat16)
        q_proj = jnp.einsum('bsd,de->bse', normed, w_query, preferred_element_type=jnp.float32)
        q_rot = rotate_pairs(q_proj.reshape(batch_local, seq_len, q_heads_local, HEAD_DIM), cos_t, sin_t).astype(jnp.bfloat16)
        kv_proj = jnp.einsum('bsd,de->bse', normed, w_kv, preferred_element_type=jnp.float32)
        k_rot = rotate_pairs(kv_proj[:, :, None, :HEAD_DIM], cos_t, sin_t)[:, :, 0, :].astype(jnp.bfloat16)
        v_head = kv_proj[:, :, HEAD_DIM:].astype(jnp.bfloat16)
        scores = jnp.einsum('bqjh,bkh->bjqk', q_rot, k_rot, preferred_element_type=jnp.float32) * SCORE_SCALE
        causal = jnp.arange(seq_len)[:, None] >= jnp.arange(seq_len)[None, :]
        attn_probs = jax.nn.softmax(jnp.where(causal, scores, MASK_VALUE), axis=-1)
        probs_bf16 = attn_probs.astype(jnp.bfloat16)
        attn_heads = jnp.einsum('bjqk,bkh->bqjh', probs_bf16, v_head, preferred_element_type=jnp.float32).astype(jnp.bfloat16)
        attn_flat = attn_heads.reshape(batch_local, seq_len, q_heads_local * HEAD_DIM)
        out_part = jnp.einsum('bse,ed->bsd', attn_flat, w_out, preferred_element_type=jnp.float32)
        attn_sum = lax.psum(out_part, 'tp')
        block_out = (hidden_f32 + attn_sum).astype(jnp.bfloat16)

        grad_w_out = jnp.einsum('bse,bsd->ed', attn_flat, grad_out, preferred_element_type=jnp.float32)
        grad_heads = jnp.einsum('bsd,ed->bse', grad_out, w_out, preferred_element_type=jnp.float32).astype(jnp.bfloat16).reshape(batch_local, seq_len, q_heads_local, HEAD_DIM)
        grad_probs = jnp.einsum('bqjh,bkh->bjqk', grad_heads, v_head, preferred_element_type=jnp.float32)
        grad_v = jnp.einsum('bjqk,bqjh->bkh', probs_bf16, grad_heads, preferred_element_type=jnp.float32)
        row_dot = jnp.sum(attn_probs * grad_probs, axis=-1, keepdims=True)
        grad_scores = (attn_probs * (grad_probs - row_dot) * SCORE_SCALE).astype(jnp.bfloat16)
        grad_q_rot = jnp.einsum('bjqk,bkh->bqjh', grad_scores, k_rot, preferred_element_type=jnp.float32)
        grad_k_rot = jnp.einsum('bjqk,bqjh->bkh', grad_scores, q_rot, preferred_element_type=jnp.float32)
        grad_q = rotate_pairs(grad_q_rot, cos_t, -sin_t).astype(jnp.bfloat16).reshape(batch_local, seq_len, q_heads_local * HEAD_DIM)
        grad_k = rotate_pairs(grad_k_rot[:, :, None, :], cos_t, -sin_t)[:, :, 0, :]
        grad_kv = jnp.concatenate([grad_k, grad_v], axis=-1).astype(jnp.bfloat16)
        grad_w_query = jnp.einsum('bsd,bse->de', normed, grad_q, preferred_element_type=jnp.float32)
        grad_w_kv_part = jnp.einsum('bsd,bse->de', normed, grad_kv, preferred_element_type=jnp.float32)
        grad_normed_part = (jnp.einsum('bse,de->bsd', grad_q, w_query, preferred_element_type=jnp.float32)
                            + jnp.einsum('bse,de->bsd', grad_kv, w_kv, preferred_element_type=jnp.float32))
        grad_normed = lax.psum(grad_normed_part, 'tp')
        gain_grad_rows = grad_normed * gain_f32
        grad_hidden = (grad_out.astype(jnp.float32) + inv_rms * (gain_grad_rows - unit_rows * jnp.mean(gain_grad_rows * unit_rows, axis=-1, keepdims=True))).astype(jnp.bfloat16)
        grad_gain = jnp.sum(grad_normed * unit_rows, axis=(0, 1))
        grad_w_kv = group_sum(grad_w_kv_part, tp_size, group_size)
        return block_out, grad_hidden, grad_gain, grad_w_query, grad_w_kv[:, :HEAD_DIM], grad_w_kv[:, HEAD_DIM:], grad_w_out

    act_spec = P('dp', None, None)
    return jax.shard_map(
        block_fn, mesh=mesh,
        in_specs=(act_spec, act_spec, P(None), P(None, 'tp'), P(None, None), P(None, None), P('tp', None)),
        out_specs=(act_spec, act_spec, P('dp'), P('dp', 'tp'), P('dp', 'tp'), P('dp', 'tp'), P(('dp', 'tp'), None)),
        check_vma=False)
```

profile of v0, /device:TPU:0, one launch (start us, length us, event | category | flops | bytes accessed | tf_op | source)
XLA Modules:
  0.0 1443.2 jit_solution(7268904220492942989)
XLA Ops:
  7.2 4.1 iota_compare_fusion
  12.1 7.2 fusion.11
  19.3 2.9 fusion.79
  24.1 9.5 fusion.41
  36.0 2.8 reshape_broadcast_in_dim.4
  38.8 2.6 fusion.91
  41.4 2.5 subtract_convert_fusion.1
  46.5 4.1 copy.28
  50.5 4.4 dot_general.68
  54.9 11.3 fusion.47
  67.9 16.0 %fusion.19 = (f32[2,2048]{1,0:T(2,128)S(1)}, f32[2048,2048,2]{1,0,2:T(8,128)}) fusion(pred[2048,2048]{0,1:T(8,128)(4,1)S(1)} %copy-done.2, bf16[2048,2,128]{0,1,2:T(2,128)(2,1)S(1)} %bitcast.157, bf16[2048,128]{0,1:T(8,128)(2,1)} %convert_element_type.117), kind=kOutput, calls=%fused_computation.27 | convolution fusion | flops 2172645376 | bytes 39337984 | tf_op jit(solution)/shard_map/bqjh,bkh->bjqk/dot_general | solution.py:64
  83.9 14.7 %fusion.18 = f32[2,2048]{1,0:T(2,128)S(1)} fusion(f32[2048,2048,2]{1,0,2:T(8,128)} %get-tuple-element.33, f32[2,2048]{1,0:T(2,128)S(1)} %get-tuple-element.32, pred[2048,2048]{0,1:T(8,128)(4,1)S(1)} %copy-done.2), kind=kLoop, calls=%fused_computation.26 | loop fusion | flops 33550336 | bytes 37781504 | tf_op jit(solution)/shard_map/reduce_sum | solution.py:66
  98.6 17.7 %fusion.50 = bf16[128,2,2048]{2,0,1:T(8,128)(2,1)S(1)} fusion(f32[1,2048,256]{1,2,0:T(8,128)} %copy-done.20, f32[2,2048]{1,0:T(2,128)S(1)} %fusion.18, f32[2,2048]{1,0:T(2,128)S(1)} %get-tuple-element.32, f32[2048,2048,2]{1,0,2:T(8,128)} %get-tuple-element.33, pred[2048,2048]{0,1:T(8,128)(4,1)} %iota_compare_fusion), kind=kOutput, calls=%fused_computation.54 | convolution fusion | flops 2189950976 | bytes 39354368 | tf_op jit(solution)/shard_map/bjqk,bkh->bqjh/dot_general | solution.py:68
  116.3 8.9 fusion.53
  126.3 25.7 %fusion.13 = (f32[2,2048]{1,0:T(2,128)S(1)}, f32[2048,2048,2]{1,0,2:T(8,128)}) fusion(f32[2,2048]{1,0:T(2,128)S(1)} %fusion.18, f32[2,2048]{1,0:T(2,128)S(1)} %get-tuple-element.32, f32[2048,2048,2]{1,0,2:T(8,128)} %get-tuple-element.33, pred[2048,2048]{0,1:T(8,128)(4,1)S(1)} %copy-done.3, bf16[2048,2,128]{0,2,1:T(8,128)(2,1)S(1)} %bitcast.159, ...), kind=kOutput, calls=%fused_computation.19 | convolution fusion | flops 2197811200 | bytes 72925184 | tf_op jit(solution)/shard_map/bqjh,bkh->bjqk/dot_general | solution.py:76
  152.0 18.3 %fusion.62 = bf16[2048,128]{0,1:T(8,128)(2,1)} fusion(bf16[2048,2,128]{0,2,1:T(8,128)(2,1)} %bitcast.160, f32[2,2048]{1,0:T(2,128)S(1)} %fusion.18, f32[2,2048]{1,0:T(2,128)S(1)} %get-tuple-element.32, f32[2048,2048,2]{1,0,2:T(8,128)} %get-tuple-element.33, pred[2048,2048]{0,1:T(8,128)(4,1)} %iota_compare_fusion), kind=kOutput, calls=%fused_computation.58 | convolution fusion | flops 2189688832 | bytes 39354368 | tf_op jit(solution)/shard_map/bjqk,bqjh->bkh/dot_general | solution.py:77
  170.3 13.5 convolution_bitcast_fusion
  183.8 29.8 %fusion.16 = bf16[1,2,2048,2048]{2,3,1,0:T(8,128)(2,1)} fusion(f32[2048,2048,2]{1,0,2:T(8,128)} %get-tuple-element.35, f32[2,2048]{1,0:T(2,128)S(1)} %get-tuple-element.34, f32[2,2048]{1,0:T(2,128)S(1)} %fusion.18, f32[2,2048]{1,0:T(2,128)S(1)} %get-tuple-element.32, f32[2048,2048,2]{1,0,2:T(8,128)} %get-tuple-element.33, pred[2048,2048]{0,1:T(8,128)(4,1)} %iota_compare_fusion), kind=kLoop, calls=%fused_computation.22 | loop fusion | flops 67108864 | bytes 88129536 | tf_op jit(solution)/shard_map/convert_element_type | solution.py:79
  213.6 8.3 fusion.44
  225.0 2.0 copy.40
  228.6 13.3 fusion.92
  241.9 11.9 fusion.59
  253.8 2.4 subtract_convert_fusion
  257.6 2.0 concatenate.33
  259.6 25.1 %add_bitcast_fusion = f32[1,2048,4096]{2,1,0:T(8,128)} fusion(f32[2048,4096]{1,0:T(8,128)} %fusion.92, bf16[4096,128]{1,0:T(8,128)(2,1)S(1)} %copy-done.8, bf16[4096,128]{1,0:T(8,128)(2,1)S(1)} %copy-done.10, bf16[2048,128]{0,1:T(8,128)(2,1)} %fusion.62, bf16[2048,128]{0,1:T(8,128)(2,1)} %concatenate.33), kind=kOutput, calls=%fused_computation.23 | convolution fusion | flops 4309647360 | bytes 70254592 | tf_op jit(solution)/shard_map/bse,de->bsd/dot_general | solution.py:88
  285.9 9.9 fusion.36
  296.4 10.3 fusion.26
  306.7 14.0 fusion.34
  321.3 2.3 fusion.89
  323.6 1048.7 %all-reduce.3.cloned.1.call-done = (f32[1,2048,4096]{2,1,0:T(8,128)}, f32[1,2048,4096]{2,1,0:T(8,128)}) async-done(((f32[1,2048,4096]{2,1,0:T(8,128)}, f32[1,2048,4096]{2,1,0:T(8,128)}), (f32[1,2048,4096]{2,1,0:T(8,128)}, f32[1,2048,4096]{2,1,0:T(8,128)})) %all-reduce.3.cloned.1.call-update) | async-done | bytes 67108880 | tf_op jit(solution)/shard_map/psum | solution.py:71
  1372.4 19.3 %fusion.10 = (f32[4096]{0:T(1024)}, f32[2048]{0:T(1024)S(1)}) fusion(f32[1,2048,4096]{2,1,0:T(8,128)} %get-tuple-element.10, bf16[1,2048,4096]{2,1,0:T(8,128)(2,1)} %param.7, f32[2048]{0:T(1024)S(1)} %copy-done.25, f32[4096]{0:T(1024)S(1)} %copy-done.23), kind=kLoop, calls=%fused_computation.13 | loop fusion | flops 58714112 | bytes 50380800 | tf_op jit(solution)/shard_map/reduce_sum | solution.py:92
  1391.7 44.3 %fusion.9 = (bf16[1,2048,4096]{2,1,0:T(8,128)(2,1)}, bf16[1,2048,4096]{2,1,0:T(8,128)(2,1)}) fusion(bf16[1,2048,4096]{2,1,0:T(8,128)(2,1)} %param.7, bf16[1,2048,4096]{2,1,0:T(8,128)(2,1)} %param.8, f32[1,2048,4096]{2,1,0:T(8,128)} %get-tuple-element.10, f32[2048]{0:T(1024)S(1)} %broadcast_multiply_fusion, f32[4096]{0:T(1024)S(1)} %copy-done.23, ...), kind=kLoop, calls=%fused_computation.12 | loop fusion | flops 92274688 | bytes 134250496 | tf_op jit(solution)/shard_map/convert_element_type | solution.py:91
  (83 shorter events, 18.4 us)
Async XLA Ops:
  7.2 109.1 %copy-start = (bf16[256,4096]{1,0:T(8,128)(2,1)S(1)}, bf16[256,4096]{1,0:T(8,128)(2,1)}, u32[]{:S(2)}) copy-start(bf16[256,4096]{1,0:T(8,128)(2,1)} %param.13) | copy-start | bytes 6291460
  7.2 1365.2 %all-reduce.3.cloned.1.call-start = ((), (), s32[]{:S(2)}) async-start(), calls=%async_computation | async-start | bytes 134217728 | tf_op jit(solution)/shard_map/psum | solution.py:71
  11.4 30.0 %copy-start.26 = (f32[64]{0:T(128)}, f32[64]{0:T(128)S(1)}, u32[]{:S(2)}) copy-start(f32[64]{0:T(128)S(1)} %multiply_power_fusion) | copy-start | bytes 772
  12.1 42.8 %copy-start.22 = (f32[4096]{0:T(1024)}, f32[4096]{0:T(1024)S(1)}, u32[]{:S(2)}) copy-start(f32[4096]{0:T(1024)S(1)} %convert_element_type.115) | copy-start | bytes 49156
  19.3 35.6 %copy-start.24 = (f32[2048]{0:T(1024)}, f32[2048]{0:T(1024)S(1)}, u32[]{:S(2)}) copy-start(f32[2048]{0:T(1024)S(1)} %add_rsqrt_fusion) | copy-start | bytes 24580
  22.2 44.1 %copy-start.5 = (f32[2048,64]{0,1:T(8,128)}, f32[2048,64]{0,1:T(8,128)S(1)}, u32[]{:S(2)}) copy-start(f32[2048,64]{0,1:T(8,128)S(1)} %get-tuple-element.31) | copy-start | bytes 1572868
  24.1 9.5 copy-start.7
  24.1 9.5 copy-start.9
  33.6 1.3 copy-start.20
  54.9 11.4 copy-start.14
  54.9 12.9 copy-start.2
  67.9 16.0 %copy-start.17 = (bf16[1,2048,2,64,2]{1,2,4,3,0:T(2,128)(2,1)}, bf16[1,2048,2,64,2]{1,2,4,3,0:T(2,128)(2,1)S(1)}, u32[]{:S(2)}) copy-start(bf16[1,2048,2,64,2]{1,2,4,3,0:T(2,128)(2,1)S(1)} %copy.76) | copy-start | bytes 3145732
  116.3 54.0 %copy-start.15 = (bf16[128,2,2048]{2,0,1:T(8,128)(2,1)}, bf16[128,2,2048]{2,0,1:T(8,128)(2,1)S(1)}, u32[]{:S(2)}) copy-start(bf16[128,2,2048]{2,0,1:T(8,128)(2,1)S(1)} %fusion.50) | copy-start | bytes 3145732
  116.3 10.0 copy-start.3
  116.3 9.9 copy-start.21
  125.3 1.0 copy-start.28
  183.8 29.8 %copy-start.11 = (bf16[2048,128,1]{0,1,2:T(8,128)(2,1)S(1)}, bf16[2048,128,1]{0,1,2:T(8,128)(2,1)}, u32[]{:S(2)}) copy-start(bf16[2048,128,1]{0,1,2:T(8,128)(2,1)} %reshape.507) | copy-start | bytes 1572868
  213.6 10.1 copy-start.6
  213.6 10.1 copy-start.13
  213.6 14.9 %copy-start.4 = (bf16[4096,256]{1,0:T(8,128)(2,1)S(1)}, bf16[4096,256]{1,0:T(8,128)(2,1)}, u32[]{:S(2)}) copy-start(bf16[4096,256]{1,0:T(8,128)(2,1)} %param.10) | copy-start | bytes 6291460
  228.6 13.3 copy-start.18
  241.9 11.9 copy-start.27
  241.9 17.7 %copy-start.8 = (bf16[4096,128]{1,0:T(8,128)(2,1)S(1)}, bf16[4096,128]{1,0:T(8,128)(2,1)}, u32[]{:S(2)}) copy-start(bf16[4096,128]{1,0:T(8,128)(2,1)} %copy-done.7) | copy-start | bytes 3145732
  241.9 17.7 %copy-start.10 = (bf16[4096,128]{1,0:T(8,128)(2,1)S(1)}, bf16[4096,128]{1,0:T(8,128)(2,1)}, u32[]{:S(2)}) copy-start(bf16[4096,128]{1,0:T(8,128)(2,1)} %copy-done.9) | copy-start | bytes 3145732
  284.7 1.0 copy-start.12
  284.7 1.2 copy-start.19
  284.7 1.2 copy-start.23
  284.7 1.2 copy-start.25
  285.9 10.5 copy-start.16
  295.8 25.0 %collective-permute-start = (f32[4096,256]{1,0:T(8,128)S(1)}, f32[4096,256]{1,0:T(8,128)S(1)}, u32[]{:S(2)}, u32[]{:S(2)}) collective-permute-start(f32[4096,256]{1,0:T(8,128)S(1)} %fusion.36), channel_id=1, source_target_pairs={{0,1},{1,0},{2,3},{3,2},{4,5},{5,4},{6,7},{7,6},{8,9},{9,8},{10,11... | collective-permute-start | bytes 12582920 | tf_op jit(solution)/shard_map/ppermute | solution.py:36
  1391.7 44.3 %copy-start.1 = (bf16[256,4096]{1,0:T(8,128)(2,1)S(1)}, bf16[256,4096]{1,0:T(8,128)(2,1)}, u32[]{:S(2)}) copy-start(bf16[256,4096]{1,0:T(8,128)(2,1)} %param.13) | copy-start | bytes 6291460
Sparse Core Ops, SparseCore 0:
  284.9 1087.4 all-reduce.2
where the time goes:
time: 1450 us; the launch traced here: 1440 us
  waiting for transfers between devices  1050 us (72%)
  matrix products  214 us (15%)
  other arithmetic  130 us (9%)
  local copies, waits for them, and re-layouts  34.9 us (2%)
  between operations  14.9 us (1%)
    psum x1, waiting for transfers between devices, block_fn(): attn_sum = lax.psum(out_part, 'tp')  1050 us
    convert_element_type x1, other arithmetic, block_fn(): (grad_out.astype(jnp.float32) + inv_rms * (gain_grad_rows - unit_rows * j...  44.3 us
    convert_element_type x1, other arithmetic, block_fn(): (attn_probs * (grad_probs - row_dot) * SCORE_SCALE).astype(jnp.bfloat16)  29.8 us
  transfers between devices with their start and end apart: 2, of which 1 were waited for; matrix products, arithmetic and copies ran while one was open for 3% of the time, Pallas kernels for 0%

commit v1 on v0

v1 whole, which is shorter than its diff:
```python
import functools
import math
import jax
import jax.numpy as jnp
from jax import lax
from jax.experimental import pallas as pl
from jax.experimental.pallas import tpu as pltpu
from jax.sharding import PartitionSpec as P

HEAD_DIM = 128
ROPE_BASE = 10000.0
MASK_VALUE = -1.0e30
SCORE_SCALE = 1.0 / math.sqrt(HEAD_DIM)

F32, BF16 = jnp.float32, jnp.bfloat16
MESH = pl.DeviceIdType.MESH
NORM_EPS = 1.0e-5
CR, CC = 8, 2048
D_MODEL = 4096
SHARD = 128
HALVES = D_MODEL // CC
PER = SHARD // CR * HALVES
R = 2 * PER
OWN, CSEND, YSEND, CONV = 4, 7, 8, 9
LAG = 3
NI = R + CONV + LAG + 1
DP, DR, D, DS = 8, 8, 16, 4


def comm_kernel(p0, p1, x_hbm, dout_hbm, gain_ref, out0, out1, gain_out,
                pbuf, upb, dnb, zb, yb, cz, cy, fb, xo, do, stage, gacc,
                psem, up_r, dn_r, z_r, y_r, cz_r, cy_r,
                up_s, dn_s, zu_s, zd_s, y_s, c_s, o_sem, l_sem):
    dp = lax.axis_index("dp")
    t = lax.axis_index("tp")
    z, y, c = t // 4, (t // 2) % 2, t % 2
    j = t % 4

    def dev(zz, yy, cc):
        return (dp, zz * 4 + yy * 2 + cc)

    def remote(src, dst, ss, rs, device):
        return pltpu.make_async_remote_copy(src_ref=src, dst_ref=dst, send_sem=ss, recv_sem=rs,
                                            device_id=device, device_id_type=MESH)

    def rowcol(r):
        kk = lax.rem(r, PER)
        return kk // HALVES, pl.multiple_of(lax.rem(kk, HALVES) * CC, CC)

    def p_copy(p, r):
        rr, cc = rowcol(r)
        return pltpu.make_async_copy(p.at[:, rr, :, pl.ds(cc, CC)], pbuf.at[lax.rem(r, DP)], psem.at[lax.rem(r, DP)])

    def p_start(r):
        @pl.when(r < PER)
        def _():
            p_copy(p0, r).start()

        @pl.when((r >= PER) & (r < R))
        def _():
            p_copy(p1, r).start()

    def up_copy(r, o, i):
        s = lax.rem(r, DR)
        return remote(upb.at[s, o], upb.at[s, o], up_s.at[o, lax.rem(i, DS)], up_r.at[o, s], dev(lax.rem(z + 1, 4), y, c))

    def up_first(r, o, i):
        s = lax.rem(r, DR)
        return remote(pbuf.at[lax.rem(r, DP), o], upb.at[s, o], up_s.at[o, lax.rem(i, DS)], up_r.at[o, s], dev(lax.rem(z + 1, 4), y, c))

    def dn_copy(r, o, i):
        s = lax.rem(r, DR)
        return remote(dnb.at[s, o], dnb.at[s, o], dn_s.at[o, lax.rem(i, DS)], dn_r.at[o, s], dev(lax.rem(z + 3, 4), y, c))

    def dn_first(r, o, i):
        s = lax.rem(r, DR)
        return remote(pbuf.at[lax.rem(r, DP), o], dnb.at[s, o], dn_s.at[o, lax.rem(i, DS)], dn_r.at[o, s], dev(lax.rem(z + 3, 4), y, c))

    def zu_copy(r, q, i):
        s = lax.rem(r, D)
        return remote(zb.at[s, q], zb.at[s, q], zu_s.at[q, lax.rem(i, DS)], z_r.at[q, s], dev(lax.rem(z + 1, 4), y, c))

    def zd_copy(r, q, i):
        s = lax.rem(r, D)
        return remote(zb.at[s, q], zb.at[s, q], zd_s.at[q, lax.rem(i, DS)], z_r.at[q, s], dev(lax.rem(z + 3, 4), y, c))

    def y_copy(r, q, i):
        s = lax.rem(r, D)
        return remote(zb.at[s, q], yb.at[s, q], y_s.at[q, lax.rem(i, DS)], y_r.at[q, s], dev(z, 1 - y, c))

    def cz_copy(r, i):
        s = lax.rem(r, D)
        return remote(zb.at[s], cz.at[s], c_s.at[0, lax.rem(i, DS)], cz_r.at[s], dev(z, y, 1 - c))

    def cy_copy(r, i):
        s = lax.rem(r, D)
        return remote(yb.at[s], cy.at[s], c_s.at[1, lax.rem(i, DS)], cy_r.at[s], dev(z, y, 1 - c))

    bufs = (zb, yb, cz, cy)

    def src_j(k):
        yy = y if k in (0, 2) else 1 - y
        cc = c if k in (0, 1) else 1 - c
        return yy * 2 + cc

    def o_copy(out, r, i, k):
        rr, cc = rowcol(r)
        b = lax.rem(i, 2)
        return pltpu.make_async_copy(stage.at[b, k], out.at[src_j(k), :, rr, :, pl.ds(cc, CC)], o_sem.at[b, k])

    def when_up(i, f):
        r = i - z
        for o in range(1, 4):
            @pl.when((r >= 0) & (r < R) & (z < o))
            def _():
                @pl.when(z == 0)
                def _():
                    f(up_first(r, o, i))

                @pl.when(z > 0)
                def _():
                    f(up_copy(r, o, i))

    def when_dn(i, f):
        r = i - 3 + z
        for o in range(0, 3):
            @pl.when((r >= 0) & (r < R) & (z > o))
            def _():
                @pl.when(z == 3)
                def _():
                    f(dn_first(r, o, i))

                @pl.when(z < 3)
                def _():
                    f(dn_copy(r, o, i))

    def when_ag(i, q, f):
        r = i - OWN - jnp.abs(z - q)
        ok = (r >= 0) & (r <= R)

        @pl.when(ok & (z >= q) & (z < 3))
        def _():
            f(zu_copy(r, q, i))

        @pl.when(ok & (z <= q) & (z > 0))
        def _():
            f(zd_copy(r, q, i))

        @pl.when(ok)
        def _():
            f(y_copy(r, q, i))

    def when_c(i, f):
        @pl.when((i - CSEND >= 0) & (i - CSEND <= R))
        def _():
            f(cz_copy(i - CSEND, i))

        @pl.when((i - YSEND >= 0) & (i - YSEND <= R))
        def _():
            f(cy_copy(i - YSEND, i))

    base = (j * 4 + z) * (SHARD // CR)
    lx = pltpu.make_async_copy(x_hbm.at[pl.ds(base, SHARD // CR)], xo, l_sem.at[0])
    ld = pltpu.make_async_copy(dout_hbm.at[pl.ds(base, SHARD // CR)], do, l_sem.at[1])
    p_start(0)
    p_start(1)
    lx.start()
    ld.start()
    gacc[...] = jnp.zeros_like(gacc)
    lx.wait()
    ld.wait()

    def body(i, _):
        ip = i - LAG

        @pl.when(ip >= 0)
        def _():
            when_up(ip, lambda cp: cp.wait_send())
            when_dn(ip, lambda cp: cp.wait_send())
            for q in range(4):
                when_ag(ip, q, lambda cp: cp.wait_send())
            when_c(ip, lambda cp: cp.wait_send())

        p_start(i + 2)

        @pl.when(i < R)
        def _():
            p_copy(p0, i).wait()

        ru = i - z
        rd = i - 3 + z

        @pl.when((ru >= 0) & (ru < R) & (z > 0))
        def _():
            for o in range(1, 4):
                @pl.when(z <= o)
                def _():
                    up_copy(ru, o, i).wait_recv()

                @pl.when(z < o)
                def _():
                    upb[lax.rem(ru, DR), o] += pbuf[lax.rem(ru, DP), o]

        @pl.when((rd >= 0) & (rd < R) & (z < 3))
        def _():
            for o in range(0, 3):
                @pl.when(z >= o)
                def _():
                    dn_copy(rd, o, i).wait_recv()

                @pl.when(z > o)
                def _():
                    dnb[lax.rem(rd, DR), o] += pbuf[lax.rem(rd, DP), o]

        rf = i - 3

        @pl.when((rf >= 0) & (rf < R))
        def _():
            fs = lax.rem(rf, 2)
            fb[fs] = pbuf[lax.rem(rf, DP), z]

            @pl.when(z > 0)
            def _():
                fb[fs] += upb[lax.rem(rf, DR), z]

            @pl.when(z < 3)
            def _():
                fb[fs] += dnb[lax.rem(rf, DR), z]

            rr, cc = rowcol(rf)

            @pl.when(rf < PER)
            def _():
                zb[lax.rem(rf, D), z] = (xo[rr, :, pl.ds(cc, CC)].astype(F32) + fb[fs]).astype(BF16).astype(F32)

            @pl.when((rf >= PER) & (fs == 1))
            def _():
                xr = xo[rr].astype(F32)
                inv = lax.rsqrt(jnp.mean(xr * xr, axis=-1, keepdims=True) + NORM_EPS)
                u = xr * inv
                dn = jnp.concatenate([fb[0], fb[1]], axis=1)
                gg = dn * gain_ref[...]
                m = jnp.mean(gg * u, axis=-1, keepdims=True)
                dx = (do[rr].astype(F32) + inv * (gg - u * m)).astype(BF16).astype(F32)
                gacc[...] += dn * u
                zb[lax.rem(rf - 1, D), z] = dx[:, :CC]
                zb[lax.rem(rf, D), z] = dx[:, CC:]

        @pl.when(rf == R)
        def _():
            zb[R % D, z] = jnp.concatenate(
                [jnp.sum(gacc[...], axis=0, keepdims=True).reshape(HALVES, CC), jnp.zeros((CR - HALVES, CC), F32)], axis=0)

        when_up(i, lambda cp: cp.start())
        when_dn(i, lambda cp: cp.start())

        for q in range(4):
            r = i - OWN - jnp.abs(z - q)

            @pl.when((r >= 0) & (r <= R) & (z != q))
            def _():
                zu_copy(r, q, i).wait_recv()

            when_ag(i, q, lambda cp: cp.start())

        @pl.when((i - YSEND >= 0) & (i - YSEND <= R))
        def _():
            for q in range(4):
                y_copy(i - YSEND, q, i).wait_recv()

        when_c(i, lambda cp: cp.start())

        io = i - 2
        ro = io - CONV
        for k in range(4):
            @pl.when((ro >= 0) & (ro < R))
            def _():
                o_copy(out0, ro, io, k).wait()

        rc = i - CONV

        @pl.when((rc >= 0) & (rc <= R))
        def _():
            cz_copy(rc, i).wait_recv()
            cy_copy(rc, i).wait_recv()

        @pl.when((rc >= 0) & (rc < R))
        def _():
            b = lax.rem(i, 2)
            s = lax.rem(rc, D)
            for k in range(4):
                for q in range(4):
                    stage[b, k, q] = bufs[k][s, q].astype(BF16)
            for k in range(4):
                @pl.when(rc < PER)
                def _():
                    o_copy(out0, rc, i, k).start()

                @pl.when(rc >= PER)
                def _():
                    o_copy(out1, rc, i, k).start()

        @pl.when(rc == R)
        def _():
            acc = jnp.zeros((CR, CC), F32)
            for k in range(4):
                for q in range(4):
                    acc = acc + bufs[k][R % D, q]
            gain_out[...] = acc
        return 0

    lax.fori_loop(0, NI, body, 0)


def comm(p0, p1, x, dout, gain):
    anyspec = pl.BlockSpec(memory_space=pl.ANY)
    vm = pl.BlockSpec(memory_space=pltpu.VMEM)
    dma = pltpu.SemaphoreType.DMA
    ch = (CR, CC)
    return pl.pallas_call(
        comm_kernel,
        out_shape=(jax.ShapeDtypeStruct((4, 4, SHARD // CR, CR, D_MODEL), BF16),
                   jax.ShapeDtypeStruct((4, 4, SHARD // CR, CR, D_MODEL), BF16),
                   jax.ShapeDtypeStruct((CR, CC), F32)),
        in_specs=[anyspec, anyspec, anyspec, anyspec, vm],
        out_specs=(anyspec, anyspec, vm),
        scratch_shapes=[
            pltpu.VMEM((DP, 4) + ch, F32), pltpu.VMEM((DR, 4) + ch, F32), pltpu.VMEM((DR, 4) + ch, F32),
            pltpu.VMEM((D, 4) + ch, F32), pltpu.VMEM((D, 4) + ch, F32), pltpu.VMEM((D, 4) + ch, F32), pltpu.VMEM((D, 4) + ch, F32),
            pltpu.VMEM((2,) + ch, F32),
            pltpu.VMEM((SHARD // CR, CR, D_MODEL), BF16), pltpu.VMEM((SHARD // CR, CR, D_MODEL), BF16),
            pltpu.VMEM((2, 4, 4) + ch, BF16), pltpu.VMEM((CR, D_MODEL), F32),
            dma((DP,)), dma((4, DR)), dma((4, DR)), dma((4, D)), dma((4, D)), dma((D,)), dma((D,)),
            dma((4, DS)), dma((4, DS)), dma((4, DS)), dma((4, DS)), dma((4, DS)), dma((2, DS)), dma((2, 4)), dma((2,)),
        ],
        compiler_params=pltpu.CompilerParams(has_side_effects=True, vmem_limit_bytes=60 * 1024 * 1024),
        name="comm",
    )(p0, p1, x, dout, gain)


def rope_tables(seq_len):
    positions = jnp.arange(seq_len, dtype=jnp.float32)
    inv_freq = ROPE_BASE ** (-jnp.arange(0, HEAD_DIM, 2, dtype=jnp.float32) / HEAD_DIM)
    angles = positions[:, None] * inv_freq[None, :]
    return jnp.cos(angles), jnp.sin(angles)


def rotate_pairs(tensor, cos_t, sin_t):
    pair_view = tensor.reshape(tensor.shape[:-1] + (HEAD_DIM // 2, 2))
    even_part = pair_view[..., 0]
    odd_part = pair_view[..., 1]
    cos_b = cos_t[:, None, :]
    sin_b = sin_t[:, None, :]
    rotated = jnp.stack([even_part * cos_b - odd_part * sin_b, even_part * sin_b + odd_part * cos_b], axis=-1)
    return rotated.reshape(tensor.shape)


def round_kernel(v_ref, o_ref):
    o_ref[...] = v_ref[...].astype(BF16)


def rounded(v):
    rows, cols = v.shape
    br = min(rows, 256)
    bc = min(cols, 1024)
    spec = pl.BlockSpec((br, bc), lambda i, k: (i, k))
    return pl.pallas_call(round_kernel, grid=(rows // br, cols // bc), in_specs=[spec], out_specs=spec,
                          out_shape=jax.ShapeDtypeStruct(v.shape, BF16), name='rounded')(v)


def solution(mesh):
    tp_size = mesh.shape['tp']
    flip = {d: [(s, s ^ d) for s in range(tp_size)] for d in (1, 2, 3)}
    swap = [(0, 1), (1, 0)]

    def block_fn(hidden, grad_out, norm_gain, w_query, w_key, w_value, w_out):
        seq_len, d_model = hidden.shape[1:]
        x, dout = hidden[0], grad_out[0]
        t = lax.axis_index('tp')
        dp = lax.axis_index('dp')
        kv_index = t // 2
        rows = seq_len // 4
        j = t % 4

        def flip_tp(v, d):
            return lax.ppermute(v, 'tp', flip[d])

        def partner_weights(w2):
            mine = lax.dynamic_index_in_dim(w2, dp, 0, keepdims=False)
            first = flip_tp(mine, 2)
            second = lax.ppermute(first, 'dp', swap)
            return first, second

        wo2 = w_out.astype(F32).reshape(2, HEAD_DIM, d_model)
        wq2 = jnp.moveaxis(w_query.astype(F32).reshape(d_model, 2, HEAD_DIM), 1, 0)
        wo_y = partner_weights(wo2)
        wq_y = partner_weights(wq2)
        wo_c = flip_tp(w_out.astype(F32), 1)
        wq_c = flip_tp(w_query.astype(F32), 1)
        wo_yc = [flip_tp(v, 1) for v in wo_y]
        wq_yc = [flip_tp(v, 1) for v in wq_y]
        wo8 = jnp.concatenate([w_out, rounded(wo_c)] + [rounded(v) for v in list(wo_y) + wo_yc], axis=0)
        kv_pair = (t // 4) * 2
        wk_own = lax.dynamic_slice_in_dim(w_key, kv_index * HEAD_DIM, HEAD_DIM, axis=1)
        wv_own = lax.dynamic_slice_in_dim(w_value, kv_index * HEAD_DIM, HEAD_DIM, axis=1)
        wk_par = lax.dynamic_slice_in_dim(w_key, (kv_index ^ 1) * HEAD_DIM, HEAD_DIM, axis=1)
        wv_par = lax.dynamic_slice_in_dim(w_value, (kv_index ^ 1) * HEAD_DIM, HEAD_DIM, axis=1)
        wq8 = jnp.concatenate([w_query, rounded(wq_c)] + [rounded(v) for v in list(wq_y) + wq_yc]
                              + [wk_own, wv_own, wk_par, wv_par], axis=1)
        w_kv = jnp.concatenate([wk_own, wv_own], axis=1)
        cos_t, sin_t = rope_tables(seq_len)

        xf = x.astype(F32)
        inv_rms = lax.rsqrt(jnp.mean(xf * xf, axis=-1, keepdims=True) + NORM_EPS)
        gain_f32 = norm_gain.astype(F32)
        normed = (xf * inv_rms * gain_f32).astype(BF16)
        q_proj = jnp.einsum('sd,de->se', normed, w_query, preferred_element_type=F32)
        q_rot = rotate_pairs(q_proj.reshape(seq_len, 2, HEAD_DIM), cos_t, sin_t).astype(BF16)
        kv_proj = jnp.einsum('sd,de->se', normed, w_kv, preferred_element_type=F32)
        k_rot = rotate_pairs(kv_proj[:, None, :HEAD_DIM], cos_t, sin_t)[:, 0, :].astype(BF16)
        v_head = kv_proj[:, HEAD_DIM:].astype(BF16)
        scores = jnp.einsum('qjh,kh->jqk', q_rot, k_rot, preferred_element_type=F32) * SCORE_SCALE
        causal = jnp.arange(seq_len)[:, None] >= jnp.arange(seq_len)[None, :]
        attn_probs = jax.nn.softmax(jnp.where(causal, scores, MASK_VALUE), axis=-1)
        probs_bf16 = attn_probs.astype(BF16)
        attn_heads = jnp.einsum('jqk,kh->qjh', probs_bf16, v_head, preferred_element_type=F32).astype(BF16)
        attn_flat = attn_heads.reshape(seq_len, 2 * HEAD_DIM)

        grad_w_out = jnp.einsum('se,sd->ed', attn_flat, dout, preferred_element_type=F32)
        grad_heads = jnp.einsum('sd,ed->se', dout, w_out, preferred_element_type=F32).astype(BF16).reshape(seq_len, 2, HEAD_DIM)
        grad_probs = jnp.einsum('qjh,kh->jqk', grad_heads, v_head, preferred_element_type=F32)
        grad_v = jnp.einsum('jqk,qjh->kh', probs_bf16, grad_heads, preferred_element_type=F32)
        row_dot = jnp.sum(attn_probs * grad_probs, axis=-1, keepdims=True)
        grad_scores = (attn_probs * (grad_probs - row_dot) * SCORE_SCALE).astype(BF16)
        grad_q_rot = jnp.einsum('jqk,kh->qjh', grad_scores, k_rot, preferred_element_type=F32)
        grad_k_rot = jnp.einsum('jqk,qjh->kh', grad_scores, q_rot, preferred_element_type=F32)
        grad_q = rotate_pairs(grad_q_rot, cos_t, -sin_t).astype(BF16).reshape(seq_len, 2 * HEAD_DIM)
        grad_k = rotate_pairs(grad_k_rot[:, None, :], cos_t, -sin_t)[:, 0, :]
        grad_kv_part = jnp.concatenate([grad_k, grad_v], axis=-1)
        grad_kv = (grad_kv_part + flip_tp(grad_kv_part, 1)).astype(BF16)
        grad_w_query = jnp.einsum('sd,se->de', normed, grad_q, preferred_element_type=F32)
        grad_w_kv = jnp.einsum('sd,se->de', normed, grad_kv, preferred_element_type=F32)

        def block(v, jj):
            return lax.dynamic_slice_in_dim(v, jj * rows, rows, axis=0)

        def heads_first(v):
            v2 = v.reshape(seq_len, 2, HEAD_DIM)
            return jnp.where(dp == 0, v2, v2[:, ::-1]).reshape(seq_len, 2 * HEAD_DIM)

        od = jnp.concatenate([attn_flat, grad_q], axis=1)
        od_first = jnp.concatenate([heads_first(attn_flat), heads_first(grad_q)], axis=1)
        od_c = flip_tp(block(od, j ^ 1).astype(F32), 1)
        od_y = flip_tp(block(od_first, j ^ 2).astype(F32), 2)
        od_yc = flip_tp(block(od_first, j ^ 3).astype(F32), 3)
        kv_y = flip_tp(block(grad_kv, j ^ 2).astype(F32), 2)
        parts = [block(od, j), rounded(od_c), rounded(od_y), rounded(od_yc)]
        e = 2 * HEAD_DIM
        o8 = jnp.concatenate([v[:, :e] for v in parts], axis=1)
        dq8 = jnp.concatenate([v[:, e:] for v in parts] + [block(grad_kv, j), rounded(kv_y)], axis=1)
        out_part = jnp.einsum('se,ed->sd', o8, wo8, preferred_element_type=F32)
        dn_part = jnp.einsum('se,de->sd', dq8, wq8, preferred_element_type=F32)

        shard = (4, SHARD // CR, CR, d_model)
        tiles = (seq_len // CR, CR, d_model)
        out, dx, gg = comm(out_part.reshape(shard), dn_part.reshape(shard), x.reshape(tiles), dout.reshape(tiles), gain_f32.reshape(1, d_model))
        return (out.reshape(1, seq_len, d_model), dx.reshape(1, seq_len, d_model), gg[:HALVES].reshape(d_model),
                grad_w_query, grad_w_kv[:, :HEAD_DIM], grad_w_kv[:, HEAD_DIM:], grad_w_out)

    act_spec = P('dp', None, None)
    return jax.shard_map(
        block_fn, mesh=mesh,
        in_specs=(act_spec, act_spec, P(None), P(None, 'tp'), P(None, None), P(None, None), P('tp', None)),
        out_specs=(act_spec, act_spec, P('dp'), P('dp', 'tp'), P('dp', 'tp'), P('dp', 'tp'), P(('dp', 'tp'), None)),
        check_vma=False)
```

time: 1450 us -> 931 us (0.64)
  waiting for transfers between devices: 1050 us -> 43.3 us
  Pallas kernels: 0 us -> 481 us
  other arithmetic: 130 us -> 39.2 us
  local copies, waits for them, and re-layouts: 34.9 us -> 110 us
  matrix products: 214 us -> 235 us
    psum x1 -> x0, waiting for transfers between devices: 1050 us -> none  [block_fn(): attn_sum = lax.psum(out_part, 'tp')]
    pallas_call x0 -> x15, Pallas kernels: none -> 481 us  [the longest x1 407 us: comm(): pl.pallas_call(comm_kernel, out_shape=(jax.ShapeDtypeStruct((4, 4, SHARD...]
    convert_element_type x5 -> x9, other arithmetic: 75 us -> 11.3 us  [the longest x1 3.31 us: block_fn(): wo_c = flip_tp(w_out.astype(F32), 1)]
    unnamed x58 -> x76, local copies, waits for them, and re-layouts: 3.56 us -> 54.8 us
    ppermute x1 -> x15, waiting for transfers between devices: 0.01 us -> 43.3 us  [the longest x13 43.1 us: flip_tp(): return lax.ppermute(v, 'tp', flip[d])]
    reduce_sum x3 -> x1, other arithmetic: 41.2 us -> 7.21 us  [block_fn(): inv_rms = lax.rsqrt(jnp.mean(xf * xf, axis=-1, keepdims=True) + NORM_EPS)]
    sub x0 -> x1, matrix products: none -> 20.6 us  [block_fn(): attn_probs = jax.nn.softmax(jnp.where(causal, scores, MASK_VALUE), axis=-1)]
    dot_general x15 -> x13, matrix products: 214 us -> 215 us  [the longest x1 43 us: block_fn(): jnp.einsum('jqk,kh->qjh', grad_scores, k_rot, preferred_element_type=F32)]
  transfers between devices with their start and end apart: 2 -> 15, of which waited for: 1 -> 4; matrix products, arithmetic and copies ran while one was open for 3% -> 35% of each run, Pallas kernels for 0% -> 8%
where the time goes in v1:
time: 931 us; the launch traced here: 921 us
  Pallas kernels  481 us (52%)
  matrix products  235 us (25%)
  local copies, waits for them, and re-layouts  110 us (12%)
  waiting for transfers between devices  43.3 us (5%)
  other arithmetic  39.2 us (4%)
  starting transfers between devices  11.9 us (1%)
    pallas_call x1, Pallas kernels, comm(): pl.pallas_call(comm_kernel, out_shape=(jax.ShapeDtypeStruct((4, 4, SHARD...  407 us
    pallas_call x14, Pallas kernels, rounded(): pl.pallas_call(round_kernel, grid=(rows // br, cols // bc), in_specs=[spe...  73.2 us
    unnamed x76, local copies, waits for them, and re-layouts  54.8 us
    ppermute x13, waiting for transfers between devices, flip_tp(): return lax.ppermute(v, 'tp', flip[d])  43.1 us
    dot_general x1, matrix products, block_fn(): jnp.einsum('jqk,kh->qjh', grad_scores, k_rot, preferred_element_type=F32)  43 us
    dot_general x1, matrix products, block_fn(): jnp.einsum('jqk,qjh->kh', grad_scores, q_rot, preferred_element_type=F32)  42.8 us
    sub x1, matrix products, block_fn(): attn_probs = jax.nn.softmax(jnp.where(causal, scores, MASK_VALUE), axis=-1)  20.6 us
  transfers between devices with their start and end apart: 15, of which 4 were waited for; matrix products, arithmetic and copies ran while one was open for 35% of the time, Pallas kernels for 8%

profile of v1, /device:TPU:0, one launch (start us, length us, event | category | flops | bytes accessed | tf_op | source)
XLA Modules:
  0.0 921.1 jit_solution(14042971645297108521)
XLA Ops:
  0.6 5.2 reshape.338
  5.9 5.2 constant_dynamic-slice_fusion
  24.2 7.2 fusion.4
  37.5 11.2 %fusion.13 = f32[2048,2,64,2]{0,2,3,1:T(8,128)} fusion(bf16[1,2048,4096]{2,1,0:T(8,128)(2,1)} %param.7, f32[4096]{0:T(1024)S(1)} %convert_element_type.112, f32[2048]{0:T(1024)S(1)} %add_rsqrt_fusion, bf16[2,64,2,4096]{3,2,1,0:T(2,128)(2,1)S(1)} %dot_general.52), kind=kOutput, calls=%fused_computation.19 | convolution fusion | flops 4328521728 | bytes 20996096 | tf_op jit(solution)/shard_map/sd,de->se/dot_general | solution.py:417
  48.7 4.1 iota_compare_fusion
  52.8 7.7 collective-permute-done.11.v_ref
  67.5 11.9 %fusion.44 = bf16[2048,256]{0,1:T(8,128)(2,1)} fusion(bf16[256,4096]{1,0:T(8,128)(2,1)} %param.13, bf16[1,2048,4096]{2,1,0:T(8,128)(2,1)} %param.8), kind=kOutput, calls=%fused_computation.45 | convolution fusion | flops 4295491584 | bytes 19922944 | tf_op jit(solution)/shard_map/sd,ed->se/dot_general | solution.py:430
  79.4 25.3 %collective-permute-done.4.v_ref = f32[128,4096]{1,0:T(8,128)} collective-permute-done((f32[128,4096]{1,0:T(8,128)}, f32[128,4096]{1,0:T(8,128)}, u32[]{:S(2)}, u32[]{:S(2)}) %collective-permute-start.4) | collective-permute-done | bytes 2097184 | tf_op jit(solution)/shard_map/ppermute | solution.py:386
  108.8 9.3 %rounded.24 = bf16[4096,128]{1,0:T(8,128)(2,1)} custom-call(f32[4096,128]{1,0:T(8,128)} %collective-permute-done.11.v_ref), custom_call_target="tpu_custom_call" | custom-call | tf_op jit(solution)/shard_map/rounded/pallas_call | solution.py:367
  118.0 3.6 rounded.18
  121.7 9.4 %rounded.25 = bf16[4096,128]{1,0:T(8,128)(2,1)} custom-call(f32[4096,128]{1,0:T(8,128)} %copy-done.14), custom_call_target="tpu_custom_call" | custom-call | tf_op jit(solution)/shard_map/rounded/pallas_call | solution.py:367
  131.5 9.8 %rounded.23 = bf16[4096,256]{1,0:T(8,128)(2,1)} custom-call(f32[4096,256]{1,0:T(8,128)} %collective-permute-done.10.v_ref), custom_call_target="tpu_custom_call" | custom-call | tf_op jit(solution)/shard_map/rounded/pallas_call | solution.py:367
  141.3 9.3 %rounded.26 = bf16[4096,128]{1,0:T(8,128)(2,1)} custom-call(f32[4096,128]{1,0:T(8,128)} %collective-permute-done.13.v_ref), custom_call_target="tpu_custom_call" | custom-call | tf_op jit(solution)/shard_map/rounded/pallas_call | solution.py:367
  156.9 3.7 rounded.19
  160.7 4.3 rounded.17
  174.9 9.3 %rounded.27 = bf16[4096,128]{1,0:T(8,128)(2,1)} custom-call(f32[4096,128]{1,0:T(8,128)} %collective-permute-done.14.v_ref), custom_call_target="tpu_custom_call" | custom-call | tf_op jit(solution)/shard_map/rounded/pallas_call | solution.py:367
  191.4 8.9 fusion.36
  208.3 14.4 %fusion.91 = f32[2048,2048,2]{1,0,2:T(8,128)} fusion(bf16[2048,2,128]{0,2,1:T(8,128)(2,1)} %bitcast.170, f32[2048,256]{0,1:T(8,128)S(1)} %copy-done.13), kind=kOutput, calls=%fused_computation.116 | convolution fusion | flops 2147483648 | bytes 35127296 | tf_op jit(solution)/shard_map/qjh,kh->jqk/dot_general | solution.py:431
  222.6 20.6 %fusion.107 = (f32[2,2048]{1,0:T(2,128)S(1)}, f32[2,2048,2048]{1,2,0:T(8,128)}) fusion(pred[2048,2048]{0,1:T(8,128)(4,1)} %iota_compare_fusion, bf16[2048,2,128]{0,1,2:T(2,128)(2,1)} %bitcast.172, bf16[2048,128]{0,1:T(8,128)(2,1)} %convert_element_type.115), kind=kOutput, calls=%fused_computation.152 | convolution fusion | flops 2181040128 | bytes 39337984 | tf_op jit(solution)/shard_map/sub | solution.py:424
  243.3 13.3 %fusion.47 = f32[2048,128]{1,0:T(8,128)S(1)} fusion(bf16[2048,2,128]{0,2,1:T(8,128)(2,1)S(1)} %bitcast.171, f32[2,2048,2048]{1,2,0:T(8,128)} %get-tuple-element.55, f32[2,2048]{1,0:T(2,128)S(1)} %get-tuple-element.54), kind=kOutput, calls=%fused_computation.46 | convolution fusion | flops 2164260864 | bytes 35667968 | tf_op jit(solution)/shard_map/jqk,qjh->kh/dot_general | solution.py:432
  256.6 12.6 %fusion.41 = bf16[128,2,2048]{2,0,1:T(8,128)(2,1)S(1)} fusion(f32[2048,256]{0,1:T(8,128)} %copy-done.12, f32[2,2048,2048]{1,2,0:T(8,128)} %get-tuple-element.55, f32[2,2048]{1,0:T(2,128)S(1)} %get-tuple-element.54), kind=kOutput, calls=%fused_computation.44 | convolution fusion | flops 2164785152 | bytes 35143680 | tf_op jit(solution)/shard_map/jqk,kh->qjh/dot_general | solution.py:426
  269.2 43.0 %fusion.40 = f32[2048,2,128]{0,2,1:T(8,128)} fusion(bf16[2048,128,1]{0,1,2:T(8,128)(2,1)S(1)} %copy-done.19, f32[2048,2048,2]{1,0,2:T(8,128)} %fusion.91, f32[2,2048,2048]{1,2,0:T(8,128)} %get-tuple-element.55, f32[2,2048]{1,0:T(2,128)S(1)} %get-tuple-element.54), kind=kOutput, calls=%fused_computation.43 | convolution fusion | flops 2206210048 | bytes 69746688 | tf_op jit(solution)/shard_map/jqk,kh->qjh/dot_general | solution.py:435
  321.1 42.8 %fusion.50 = f32[2048,1,64,2]{0,2,3,1:T(8,128)S(1)} fusion(f32[2048,2048,2]{1,0,2:T(8,128)} %fusion.91, bf16[64,2,2,2048]{3,2,1,0:T(2,128)(2,1)} %bitcast.173, f32[2,2048,2048]{1,2,0:T(8,128)} %get-tuple-element.55, f32[2,2048]{1,0:T(2,128)S(1)} %get-tuple-element.54), kind=kOutput, calls=%fused_computation.47 | convolution fusion | flops 2206210048 | bytes 69222400 | tf_op jit(solution)/shard_map/jqk,qjh->kh/dot_general | solution.py:436
  396.1 14.0 %fusion.21 = f32[4096,256]{1,0:T(8,128)} fusion(bf16[2048,256]{0,1:T(8,128)(2,1)S(1)} %convert_element_type.127, bf16[1,2048,4096]{2,1,0:T(8,128)(2,1)} %param.7, f32[4096]{0:T(1024)S(1)} %copy-done.21, f32[2048]{0:T(1024)S(1)} %copy-done.25), kind=kOutput, calls=%fused_computation.27 | convolution fusion | flops 4328521728 | bytes 22044672 | tf_op jit(solution)/shard_map/sd,se->de/dot_general | solution.py:441
  416.0 10.1 %fusion.17 = f32[256,4096]{1,0:T(8,128)} fusion(bf16[2048,256]{0,1:T(8,128)(2,1)S(1)} %bitcast.166, bf16[1,2048,4096]{2,1,0:T(8,128)(2,1)} %param.8), kind=kOutput, calls=%fused_computation.23 | convolution fusion | flops 4294967296 | bytes 22020096 | tf_op jit(solution)/shard_map/se,sd->ed/dot_general | solution.py:429
  437.2 10.3 %fusion.57 = f32[512,4096]{1,0:T(8,128)} fusion(bf16[1024,4096]{1,0:T(8,128)(2,1)} %constant_dynamic-update-slice_fusion, bf16[512,256]{1,0:T(8,128)(2,1)S(1)} %get-tuple-element.44, bf16[512,256]{1,0:T(8,128)(2,1)S(1)} %get-tuple-element.46, bf16[512,256]{1,0:T(8,128)(2,1)S(1)} %get-tuple-element.48, bf16[512,256]{1,0:T(8,128)(2,1)S(1)} %get-tuple-element.50), kind=kOutput, calls=%fused_computation.69 | convolution fusion | flops 4299161600 | bytes 17825792 | tf_op jit(solution)/shard_map/se,ed->sd/dot_general | solution.py:461
  449.4 10.5 %fusion.34 = f32[4096,256]{1,0:T(8,128)S(1)} fusion(bf16[2048,256]{1,0:T(8,128)(2,1)S(1)} %add_convert_fusion, bf16[1,2048,4096]{2,1,0:T(8,128)(2,1)} %param.7, f32[4096]{0:T(1024)S(1)} %copy-done.21, f32[2048]{0:T(1024)S(1)} %copy-done.25), kind=kOutput, calls=%fused_computation.40 | convolution fusion | flops 4328521728 | bytes 22044672 | tf_op jit(solution)/shard_map/sd,se->de/dot_general | solution.py:442
  463.8 10.1 %collective-permute-done.9.v_ref = f32[512,256]{1,0:T(8,128)S(1)} collective-permute-done((f32[512,256]{1,0:T(8,128)S(1)}, f32[512,256]{1,0:T(8,128)S(1)}, u32[]{:S(2)}, u32[]{:S(2)}) %collective-permute-start.9) | collective-permute-done | bytes 524320 | tf_op jit(solution)/shard_map/ppermute | solution.py:386
  477.4 11.7 %fusion.116 = f32[512,4096]{1,0:T(8,128)} fusion(bf16[512,1536]{1,0:T(8,128)(2,1)S(1)} %constant_dynamic-update-slice_fusion.6, bf16[4096,1536]{1,0:T(8,128)(2,1)} %dynamic-slice_dynamic-update-slice_fusion), kind=kOutput, calls=%fused_computation.153 | convolution fusion | flops 6442450944 | bytes 22544384 | tf_op jit(solution)/shard_map/se,de->sd/dot_general | solution.py:462
  489.1 407.3 %comm.1 = (bf16[4,4,16,8,4096]{4,3,2,1,0:T(8,128)(2,1)}, bf16[4,4,16,8,4096]{4,3,2,1,0:T(8,128)(2,1)}, f32[8,2048]{1,0:T(8,128)}) custom-call(f32[4,16,8,4096]{3,2,1,0:T(8,128)} %bitcast.162, f32[4,16,8,4096]{3,2,1,0:T(8,128)} %bitcast.163, bf16[256,8,4096]{2,1,0:T(8,128)(2,1)} %bitcast.156, bf16[256,8,4096]{2,1,0:T(8,128)(2,1)} %bitcast.158, ...), custom_call_target="tpu_custom_call" | custom-call | tf_op jit(solution)/shard_map/comm/pallas_call | solution.py:320
  897.8 14.9 %copy.134 = bf16[1,2048,4096]{2,1,0:T(8,128)(2,1)} copy(bf16[1,2048,4096]{2,1,0:T(8,128)(2,1)} %bitcast.160) | data formatting | bytes 33554432
  914.7 6.2 copy.135
  (154 shorter events, 132.8 us)
Async XLA Ops:
  0.6 13.4 %copy-start = (bf16[4096,256]{1,0:T(8,128)(2,1)S(1)}, bf16[4096,256]{1,0:T(8,128)(2,1)}, u32[]{:S(2)}) copy-start(bf16[4096,256]{1,0:T(8,128)(2,1)} %param.10) | copy-start | bytes 6291460
  11.0 49.5 %collective-permute-start.11 = (f32[4096,128]{1,0:T(8,128)}, f32[4096,128]{1,0:T(8,128)}, u32[]{:S(2)}, u32[]{:S(2)}) collective-permute-start(f32[4096,128]{1,0:T(8,128)} %bitcast.30), channel_id=1, source_target_pairs={{0,2},{1,3},{2,0},{3,1},{4,6},{5,7},{6,4},{7,5},{8,10},{9,11},{10,... | collective-permute-start | bytes 6291464 | tf_op jit(solution)/shard_map/ppermute | solution.py:386
  17.2 113.8 %collective-permute-start.10 = (f32[4096,256]{1,0:T(8,128)}, f32[4096,256]{1,0:T(8,128)}, u32[]{:S(2)}, u32[]{:S(2)}) collective-permute-start(f32[4096,256]{1,0:T(8,128)} %get-tuple-element.29), channel_id=1, source_target_pairs={{0,1},{1,0},{2,3},{3,2},{4,5},{5,4},{6,7},{7,6},{8,9},{9,8},{10,11... | collective-permute-start | bytes 12582920 | tf_op jit(solution)/shard_map/ppermute | solution.py:386
  20.5 140.1 %collective-permute-start.3 = (f32[256,4096]{1,0:T(8,128)}, f32[256,4096]{1,0:T(8,128)}, u32[]{:S(2)}, u32[]{:S(2)}) collective-permute-start(f32[256,4096]{1,0:T(8,128)} %get-tuple-element.31), channel_id=1, source_target_pairs={{0,1},{1,0},{2,3},{3,2},{4,5},{5,4},{6,7},{7,6},{8,9},{9,8},{10,11... | collective-permute-start | bytes 12582920 | tf_op jit(solution)/shard_map/ppermute | solution.py:386
  24.1 80.5 %collective-permute-start.4 = (f32[128,4096]{1,0:T(8,128)}, f32[128,4096]{1,0:T(8,128)}, u32[]{:S(2)}, u32[]{:S(2)}) collective-permute-start(f32[128,4096]{1,0:T(8,128)} %dynamic-slice_bitcast_fusion), channel_id=1, source_target_pairs={{0,2},{1,3},{2,0},{3,1},{4,6},{5,7},{6,4},{7,5},{8,10},{9,11},{10,... | collective-permute-start | bytes 6291464 | tf_op jit(solution)/shard_map/ppermute | solution.py:386
  24.1 167.2 %copy-start.20 = (f32[4096]{0:T(1024)}, f32[4096]{0:T(1024)S(1)}, u32[]{:S(2)}) copy-start(f32[4096]{0:T(1024)S(1)} %convert_element_type.112) | copy-start | bytes 49156
  31.4 160.0 %copy-start.24 = (f32[2048]{0:T(1024)}, f32[2048]{0:T(1024)S(1)}, u32[]{:S(2)}) copy-start(f32[2048]{0:T(1024)S(1)} %add_rsqrt_fusion) | copy-start | bytes 24580
  48.7 154.5 %copy-start.26 = (f32[64]{0:T(128)}, f32[64]{0:T(128)S(1)}, u32[]{:S(2)}) copy-start(f32[64]{0:T(128)S(1)} %multiply_power_fusion) | copy-start | bytes 772
  60.5 46.0 %collective-permute-start.12 = (f32[4096,128]{1,0:T(8,128)}, f32[4096,128]{1,0:T(8,128)S(1)}, u32[]{:S(2)}, u32[]{:S(2)}) collective-permute-start(f32[4096,128]{1,0:T(8,128)} %collective-permute-done.11.v_ref), channel_id=1, source_target_pairs={{0,16},{16,0},{1,17},{17,1},{2,18},{18,2},{3,19},{19,3},{4,20},{20... | collective-permute-start | bytes 6291464 | tf_op jit(solution)/shard_map/ppermute | solution.py:391
  65.4 13.9 %copy-start.2 = (f32[2048,64]{0,1:T(8,128)}, f32[2048,64]{0,1:T(8,128)S(1)}, u32[]{:S(2)}) copy-start(f32[2048,64]{0,1:T(8,128)S(1)} %get-tuple-element.53) | copy-start | bytes 1572868
  65.5 75.8 %collective-permute-start.13 = (f32[4096,128]{1,0:T(8,128)}, f32[4096,128]{1,0:T(8,128)}, u32[]{:S(2)}, u32[]{:S(2)}) collective-permute-start(f32[4096,128]{1,0:T(8,128)} %collective-permute-done.11.v_ref), channel_id=1, source_target_pairs={{0,1},{1,0},{2,3},{3,2},{4,5},{5,4},{6,7},{7,6},{8,9},{9,8},{10,11... | collective-permute-start | bytes 6291464 | tf_op jit(solution)/shard_map/ppermute | solution.py:386
  104.6 52.3 %collective-permute-start.5 = (f32[128,4096]{1,0:T(8,128)}, f32[128,4096]{1,0:T(8,128)}, u32[]{:S(2)}, u32[]{:S(2)}) collective-permute-start(f32[128,4096]{1,0:T(8,128)} %collective-permute-done.4.v_ref), channel_id=1, source_target_pairs={{0,16},{16,0},{1,17},{17,1},{2,18},{18,2},{3,19},{19,3},{4,20},{20... | collective-permute-start | bytes 6291464 | tf_op jit(solution)/shard_map/ppermute | solution.py:391
  106.6 11.4 %copy-start.14 = (f32[4096,128]{1,0:T(8,128)}, f32[4096,128]{1,0:T(8,128)S(1)}, u32[]{:S(2)}) copy-start(f32[4096,128]{1,0:T(8,128)S(1)} %collective-permute-done.12.v_ref) | copy-start | bytes 6291460
  106.6 58.4 %collective-permute-start.6 = (f32[128,4096]{1,0:T(8,128)}, f32[128,4096]{1,0:T(8,128)}, u32[]{:S(2)}, u32[]{:S(2)}) collective-permute-start(f32[128,4096]{1,0:T(8,128)} %collective-permute-done.4.v_ref), channel_id=1, source_target_pairs={{0,1},{1,0},{2,3},{3,2},{4,5},{5,4},{6,7},{7,6},{8,9},{9,8},{10,11... | collective-permute-start | bytes 6291464 | tf_op jit(solution)/shard_map/ppermute | solution.py:386
  121.7 32.1 %copy-start.7 = (bf16[4096,128]{1,0:T(8,128)(2,1)S(1)}, bf16[4096,128]{1,0:T(8,128)(2,1)}, u32[]{:S(2)}) copy-start(bf16[4096,128]{1,0:T(8,128)(2,1)} %rounded.24) | copy-start | bytes 3145732
  131.0 23.8 %copy-start.5 = (bf16[4096,128]{1,0:T(8,128)(2,1)S(1)}, bf16[4096,128]{1,0:T(8,128)(2,1)}, u32[]{:S(2)}) copy-start(bf16[4096,128]{1,0:T(8,128)(2,1)} %rounded.25) | copy-start | bytes 3145732
  131.0 43.9 %collective-permute-start.14 = (f32[4096,128]{1,0:T(8,128)}, f32[4096,128]{1,0:T(8,128)}, u32[]{:S(2)}, u32[]{:S(2)}) collective-permute-start(f32[4096,128]{1,0:T(8,128)} %copy-done.14), channel_id=1, source_target_pairs={{0,1},{1,0},{2,3},{3,2},{4,5},{5,4},{6,7},{7,6},{8,9},{9,8},{10,11... | collective-permute-start | bytes 6291464 | tf_op jit(solution)/shard_map/ppermute | solution.py:386
  156.9 14.9 %copy-start.4 = (bf16[128,4096]{1,0:T(8,128)(2,1)S(1)}, bf16[128,4096]{1,0:T(8,128)(2,1)}, u32[]{:S(2)}) copy-start(bf16[128,4096]{1,0:T(8,128)(2,1)} %rounded.18) | copy-start | bytes 3145732
  160.6 12.2 %copy-start.6 = (bf16[128,4096]{1,0:T(8,128)(2,1)S(1)}, bf16[128,4096]{1,0:T(8,128)(2,1)}, u32[]{:S(2)}) copy-start(bf16[128,4096]{1,0:T(8,128)(2,1)} %rounded.19) | copy-start | bytes 3145732
  160.6 249.6 %collective-permute-start.7 = (f32[128,4096]{1,0:T(8,128)}, f32[128,4096]{1,0:T(8,128)}, u32[]{:S(2)}, u32[]{:S(2)}) collective-permute-start(f32[128,4096]{1,0:T(8,128)} %collective-permute-done.5.v_ref), channel_id=1, source_target_pairs={{0,1},{1,0},{2,3},{3,2},{4,5},{5,4},{6,7},{7,6},{8,9},{9,8},{10,11... | collective-permute-start | bytes 6291464 | tf_op jit(solution)/shard_map/ppermute | solution.py:386
  222.6 20.6 %copy-start.17 = (bf16[2048,256]{0,1:T(8,128)(2,1)S(1)}, bf16[2048,256]{0,1:T(8,128)(2,1)}, u32[]{:S(2)}) copy-start(bf16[2048,256]{0,1:T(8,128)(2,1)} %fusion.44) | copy-start | bytes 3145732
  256.6 113.8 %copy-start.10 = (f32[2048,128]{1,0:T(8,128)}, f32[2048,128]{1,0:T(8,128)S(1)}, u32[]{:S(2)}) copy-start(f32[2048,128]{1,0:T(8,128)S(1)} %fusion.47) | copy-start | bytes 3145732
  256.6 12.6 %copy-start.19 = (bf16[2048,128,1]{0,1,2:T(8,128)(2,1)S(1)}, bf16[2048,128,1]{0,1,2:T(8,128)(2,1)}, u32[]{:S(2)}) copy-start(bf16[2048,128,1]{0,1,2:T(8,128)(2,1)} %reshape.348) | copy-start | bytes 1572868
  321.1 42.8 %copy-start.27 = (f32[64]{0:T(128)S(1)}, f32[64]{0:T(128)}, u32[]{:S(2)}) copy-start(f32[64]{0:T(128)} %copy-done.26) | copy-start | bytes 772
  371.9 75.6 %collective-permute-start.8 = (f32[2048,256]{1,0:T(8,128)}, f32[2048,256]{1,0:T(8,128)}, u32[]{:S(2)}, u32[]{:S(2)}) collective-permute-start(f32[2048,256]{1,0:T(8,128)} %pad_maximum_fusion), channel_id=1, source_target_pairs={{0,1},{1,0},{2,3},{3,2},{4,5},{5,4},{6,7},{7,6},{8,9},{9,8},{10,11... | collective-permute-start | bytes 6291464 | tf_op jit(solution)/shard_map/ppermute | solution.py:386
  382.0 14.0 %copy-start.21 = (f32[4096]{0:T(1024)S(1)}, f32[4096]{0:T(1024)}, u32[]{:S(2)}) copy-start(f32[4096]{0:T(1024)} %copy-done.20) | copy-start | bytes 49156
  382.0 14.0 %copy-start.25 = (f32[2048]{0:T(1024)S(1)}, f32[2048]{0:T(1024)}, u32[]{:S(2)}) copy-start(f32[2048]{0:T(1024)} %copy-done.24) | copy-start | bytes 24580
  382.0 44.1 %collective-permute-start.1 = (f32[512,512]{1,0:T(8,128)}, f32[512,512]{1,0:T(8,128)}, u32[]{:S(2)}, u32[]{:S(2)}) collective-permute-start(f32[512,512]{1,0:T(8,128)} %get-tuple-element.25), channel_id=1, source_target_pairs={{0,2},{1,3},{2,0},{3,1},{4,6},{5,7},{6,4},{7,5},{8,10},{9,11},{10,... | collective-permute-start | bytes 3145736 | tf_op jit(solution)/shard_map/ppermute | solution.py:386
  390.9 37.2 %collective-permute-start = (f32[512,512]{1,0:T(8,128)}, f32[512,512]{1,0:T(8,128)}, u32[]{:S(2)}, u32[]{:S(2)}) collective-permute-start(f32[512,512]{1,0:T(8,128)} %get-tuple-element.24), channel_id=1, source_target_pairs={{0,1},{1,0},{2,3},{3,2},{4,5},{5,4},{6,7},{7,6},{8,9},{9,8},{10,11... | collective-permute-start | bytes 3145736 | tf_op jit(solution)/shard_map/ppermute | solution.py:386
  390.9 39.1 %collective-permute-start.2 = (f32[512,512]{1,0:T(8,128)}, f32[512,512]{1,0:T(8,128)}, u32[]{:S(2)}, u32[]{:S(2)}) collective-permute-start(f32[512,512]{1,0:T(8,128)} %get-tuple-element.26), channel_id=1, source_target_pairs={{0,3},{1,2},{2,1},{3,0},{4,7},{5,6},{6,5},{7,4},{8,11},{9,10},{10,... | collective-permute-start | bytes 3145736 | tf_op jit(solution)/shard_map/ppermute | solution.py:386
  460.0 13.9 %collective-permute-start.9 = (f32[512,256]{1,0:T(8,128)S(1)}, f32[512,256]{1,0:T(8,128)S(1)}, u32[]{:S(2)}, u32[]{:S(2)}) collective-permute-start(f32[512,256]{1,0:T(8,128)S(1)} %get-tuple-element.37), channel_id=1, source_target_pairs={{0,2},{1,3},{2,0},{3,1},{4,6},{5,7},{6,4},{7,5},{8,10},{9,11},{10,... | collective-permute-start | bytes 1572872 | tf_op jit(solution)/shard_map/ppermute | solution.py:386
  897.8 16.9 %copy-start.1 = (bf16[4,4,16,8,4096]{4,3,2,1,0:T(8,128)(2,1)S(1)}, bf16[4,4,16,8,4096]{4,3,2,1,0:T(8,128)(2,1)}, u32[]{:S(2)}) copy-start(bf16[4,4,16,8,4096]{4,3,2,1,0:T(8,128)(2,1)} %get-tuple-element.11) | copy-start | bytes 50331652
  (11 other events, 64.6 us)
